TPU v7x, 32 devices: a whole 2x2x4 slice. The times are simulated.
32 devices in a mesh: blk: 16 (over z, y, core), grp: 2 (over x).
Axes of the slice: x: 2, y: 2, z: 4, core: 2. Of those that a mesh axis runs over, the one named last changes fastest.
Arguments:
- matrix_sat: float32 [512, 65536], P('grp', 'blk'), may hold values from -0.07883404 to 0.07883404
- matrix_ter: float32 [512, 65536], P('grp', 'blk'), may hold values from -0.07883404 to 0.07883404
- probes: float32 [16, 65536], P(None, 'blk'), may hold values from -6 to 6
Outputs:
- row_part: float32 [2, 16, 512], P(None, None, 'grp')
- column_part: float32 [2, 16, 65536], P(None, None, ('blk', 'grp'))
- trace_terms: float32 [2, 16], replicated
All inputs are finite; a program needn't handle non-finite values.
Results may differ from a plain program's by a relative error of at most 0.000096.
Values sent between devices are 32-bit elements; how exact they have to be, the bound alone decides.
A program may use at most 64 MiB of HBM per device.

v0:
```python
import jax
import jax.numpy as jnp
from jax import lax
from jax.sharding import PartitionSpec as P


def broadcast(block, axis, source):
    block = jnp.where(lax.axis_index(axis) == source, block, jnp.zeros_like(block))
    return lax.psum(block, axis)


def shards(matrix_sat, matrix_ter, probes):
    rows_dev, cols_dev = matrix_sat.shape
    column_index = lax.axis_index("blk")
    row_index = lax.axis_index("grp")
    row_ids = row_index * rows_dev + lax.broadcasted_iota(jnp.int32, (rows_dev, cols_dev), 0)
    col_ids = column_index * cols_dev + lax.broadcasted_iota(jnp.int32, (rows_dev, cols_dev), 1)
    upper_mask = col_ids >= row_ids
    strict_mask = col_ids > row_ids
    mine = lax.dynamic_slice_in_dim(probes, row_index * rows_dev, rows_dev, 1)
    slab_probes = broadcast(mine, "blk", 0)
    hp = lax.Precision.HIGHEST
    direct_list = []
    mirror_list = []
    for matrix in (matrix_sat, matrix_ter):
        masked_upper = jnp.where(upper_mask, matrix, 0.0)
        masked_strict = jnp.where(strict_mask, matrix, 0.0)
        direct_list.append(
            lax.dot_general(probes, masked_upper, (((1,), (1,)), ((), ())), precision=hp)
        )
        mirror_list.append(jnp.dot(slab_probes, masked_strict, precision=hp))
    direct_terms = jnp.stack(direct_list)
    mirror_terms = jnp.stack(mirror_list)
    early_local = jnp.sum(slab_probes[None] * direct_terms, axis=2) + jnp.sum(
        probes[None] * mirror_terms, axis=2
    )
    early_trace = lax.psum(early_local, ("blk", "grp"))
    row_part = lax.psum(direct_terms, "blk")
    column_part = lax.psum_scatter(mirror_terms, "grp", scatter_dimension=2, tiled=True)
    return (row_part, column_part, early_trace)


def solution(mesh):
    in_specs = (P("grp", "blk"), P("grp", "blk"), P(None, "blk"))
    out_specs = (P(None, None, "grp"), P(None, None, ("blk", "grp")), P())
    return jax.shard_map(shards, mesh=mesh, in_specs=in_specs, out_specs=out_specs, check_vma=False)
```

profile of v0, /device:TPU:14, one launch (start us, length us, event | category | flops | bytes accessed | tf_op | source)
XLA Modules:
  0.0 133.0 jit_solution(6201908092485074033)
XLA Ops:
  7.2 0.0 copy-start.2
  7.2 0.0 reduce-scatter.2.cloned.1.call-start
  7.2 0.0 copy-start
  7.3 5.8 %fusion.14 = f32[1,16,256]{2,1,0:T(8,128)S(1)} fusion(f32[16,4096]{1,0:T(8,128)} %param.5, f32[256,4096]{1,0:T(8,128)} %param.4, s32[4096]{0:T(1024)S(1)} %iota_add_fusion, s32[256]{0:T(256)S(1)} %iota_add_fusion.1), kind=kOutput, calls=%fused_computation.20 | convolution fusion | flops 203423744 | bytes 4490240 | tf_op jit(solution)/shard_map/dot_general | solution.py:29
  13.1 0.0 copy-done.2
  13.1 0.0 copy-done
  13.1 3.5 %fusion.15 = f32[1,16,256]{2,1,0:T(8,128)S(1)} fusion(f32[16,4096]{1,0:T(8,128)S(1)} %copy-done.2, f32[256,4096]{1,0:T(8,128)S(1)} %copy-done, s32[4096]{0:T(1024)S(1)} %iota_add_fusion, s32[256]{0:T(256)S(1)} %iota_add_fusion.1), kind=kOutput, calls=%fused_computation.21 | convolution fusion | flops 203423744 | bytes 4490240 | tf_op jit(solution)/shard_map/dot_general | solution.py:29
  16.6 49.1 %all-reduce = (f32[2,16,256]{2,1,0:T(8,128)}, f32[16,256]{1,0:T(8,128)S(1)}) all-reduce(f32[2,16,256]{2,1,0:T(8,128)S(1)} %pad_maximum_fusion.1, f32[16,256]{1,0:T(8,128)S(1)} %dynamic-slice_select_fusion), channel_id=1, replica_groups=mesh['blk'=16,'grp'=2] {'blk'}, use_global_device_ids=true, to_apply=%region_0.1 | all-reduce | flops 12288 | bytes 98304 | tf_op jit(solution)/shard_map/psum | solution.py:38
  65.7 0.0 copy-start.1
  65.7 4.7 %convolution_bitcast_fusion = f32[1,16,4096]{2,1,0:T(8,128)S(1)} fusion(f32[16,256]{1,0:T(8,128)S(1)} %get-tuple-element.4, f32[256,4096]{1,0:T(8,128)} %param.4, s32[4096]{0:T(1024)S(1)} %iota_add_fusion, s32[256]{0:T(256)S(1)} %iota_add_fusion.1), kind=kOutput, calls=%fused_computation.4 | convolution fusion | flops 203423744 | bytes 4490240 | tf_op jit(solution)/shard_map/dot_general | solution.py:31
  70.4 0.0 copy-done.1
  70.4 2.4 %convolution_bitcast_fusion.1 = f32[1,16,4096]{2,1,0:T(8,128)S(1)} fusion(f32[16,256]{1,0:T(8,128)S(1)} %get-tuple-element.4, f32[256,4096]{1,0:T(8,128)S(1)} %copy-done.1, s32[4096]{0:T(1024)S(1)} %iota_add_fusion, s32[256]{0:T(256)S(1)} %iota_add_fusion.1), kind=kOutput, calls=%fused_computation.5 | convolution fusion | flops 203423744 | bytes 4490240 | tf_op jit(solution)/shard_map/dot_general | solution.py:31
  72.8 0.9 multiply_reduce_fusion
  73.7 0.0 reduce-scatter.2.cloned.1.call-update
  73.7 0.1 multiply_reduce_fusion.1
  73.8 52.4 %psum.23 = f32[2,16]{1,0:T(2,128)} all-reduce(f32[2,16]{1,0:T(2,128)S(1)} %add.33), channel_id=1, replica_groups=mesh['blk'=16,'grp'=2] {'blk','grp'}, use_global_device_ids=true, to_apply=%region_5.6 | all-reduce | flops 32 | bytes 256 | tf_op jit(solution)/shard_map/psum | solution.py:37
  126.2 0.0 reduce-scatter.2.cloned.1.call-done
  (5 shorter events, 0.0 us)
Async XLA Ops:
  7.2 5.9 %copy-start.2 = (f32[16,4096]{1,0:T(8,128)S(1)}, f32[16,4096]{1,0:T(8,128)}, u32[]{:S(2)}) copy-start(f32[16,4096]{1,0:T(8,128)} %param.5) | copy-start | bytes 786436
  7.2 119.0 %reduce-scatter.2.cloned.1.call-start = ((), (), s32[]{:S(2)}) async-start(), calls=%async_computation.1 | async-start | bytes 786432 | tf_op jit(solution)/shard_map/reduce_scatter | solution.py:39
  7.2 5.9 %copy-start = (f32[256,4096]{1,0:T(8,128)S(1)}, f32[256,4096]{1,0:T(8,128)}, u32[]{:S(2)}) copy-start(f32[256,4096]{1,0:T(8,128)} %param.3) | copy-start | bytes 12582916
  65.7 4.7 %copy-start.1 = (f32[256,4096]{1,0:T(8,128)S(1)}, f32[256,4096]{1,0:T(8,128)}, u32[]{:S(2)}) copy-start(f32[256,4096]{1,0:T(8,128)} %param.3) | copy-start | bytes 12582916
Sparse Core Ops, SparseCore 0:
  73.8 24.2 reduce-scatter.1
where the time goes:
time: 133 us
  blocking collectives  101 us (76%)
  matrix products  16.3 us (12%)
  between operations  14.1 us (11%)
    psum x1, blocking collectives, shards(): early_trace = lax.psum(early_local, ('blk', 'grp'))  52.4 us
    psum x1, blocking collectives, shards(): row_part = lax.psum(direct_terms, 'blk')  49.1 us
    dot_general x2, matrix products, shards(): lax.dot_general(probes, masked_upper, (((1,), (1,)), ((), ())), precision...  9.25 us
    dot_general x2, matrix products, shards(): mirror_list.append(jnp.dot(slab_probes, masked_strict, precision=hp))  7.08 us
  transfers between devices with their start and end apart: 1, of which 0 were waited for; matrix products, arithmetic and copies ran while one was open for 0% of the time, Pallas kernels for 0%

commit v1 on v0

--- a/solution.py
+++ b/solution.py
@@ -35,7 +35,9 @@
         probes[None] * mirror_terms, axis=2
     )
     early_trace = lax.psum(early_local, ("blk", "grp"))
-    row_part = lax.psum(direct_terms, "blk")
+    row_part = direct_terms
+    for hop in (1, 2, 4, 8):
+        row_part = row_part + lax.ppermute(row_part, "blk", [(dev, dev ^ hop) for dev in range(16)])
     column_part = lax.psum_scatter(mirror_terms, "grp", scatter_dimension=2, tiled=True)
     return (row_part, column_part, early_trace)
 

time: 133 us -> 145 us (1.090); the launches traced: 133 us -> 143 us
  starting transfers between devices: 0.04 us -> 14.2 us
  blocking collectives: 101 us -> 90.6 us
  waiting for transfers between devices: 0.02 us -> 5 us
    ppermute x0 -> x4, starting transfers between devices: none -> 14.2 us  [shards(): lax.ppermute(row_part, 'blk', [(dev, dev ^ hop) for dev in range(16)])]
    psum x1, blocking collectives: 52.4 us -> 41.6 us  [shards(): early_trace = lax.psum(early_local, ('blk', 'grp'))]
    ppermute x0 -> x4, waiting for transfers between devices: none -> 4.98 us  [shards(): lax.ppermute(row_part, 'blk', [(dev, dev ^ hop) for dev in range(16)])]
  transfers between devices with their start and end apart: 1 -> 5, of which waited for: 0 -> 3; matrix products, arithmetic and copies ran while one was open for 0% -> 7% of each run, Pallas kernels for 0% -> 0%
where the time goes in v1:
time: 145 us; the launch traced here: 143 us
  blocking collectives  90.6 us (62%)
  matrix products  16.3 us (11%)
  starting transfers between devices  14.2 us (10%)
  between operations  14.1 us (10%)
  waiting for transfers between devices  5 us (3%)
  other arithmetic  2.34 us (2%)
    psum x1, blocking collectives, broadcast(): return lax.psum(block, axis)  49 us
    psum x1, blocking collectives, shards(): early_trace = lax.psum(early_local, ('blk', 'grp'))  41.6 us
    ppermute x4, starting transfers between devices, shards(): lax.ppermute(row_part, 'blk', [(dev, dev ^ hop) for dev in range(16)])  14.2 us
    dot_general x2, matrix products, shards(): lax.dot_general(probes, masked_upper, (((1,), (1,)), ((), ())), precision...  9.23 us
    dot_general x2, matrix products, shards(): mirror_list.append(jnp.dot(slab_probes, masked_strict, precision=hp))  7.08 us
    ppermute x4, waiting for transfers between devices, shards(): lax.ppermute(row_part, 'blk', [(dev, dev ^ hop) for dev in range(16)])  4.98 us
  transfers between devices with their start and end apart: 5, of which 3 were waited for; matrix products, arithmetic and copies ran while one was open for 7% of the time, Pallas kernels for 0%

profile of v1, /device:TPU:14, one launch (start us, length us, event | category | flops | bytes accessed | tf_op | source)
XLA Modules:
  0.0 142.6 jit_solution(14861866257701781627)
XLA Ops:
  7.2 0.0 reduce-scatter.2.cloned.1.call-start
  7.2 0.7 dynamic-slice_select_fusion
  8.0 49.0 %psum.14 = f32[16,256]{1,0:T(8,128)S(1)} all-reduce(f32[16,256]{1,0:T(8,128)S(1)} %dynamic-slice_select_fusion), channel_id=1, replica_groups=mesh['blk'=16,'grp'=2] {'blk'}, use_global_device_ids=true, to_apply=%region_0.1 | all-reduce | flops 4096 | bytes 32768 | tf_op jit(solution)/shard_map/psum | solution.py:9
  57.0 0.0 copy-start
  57.0 0.0 copy-start.2
  57.0 4.7 %convolution_bitcast_fusion.1 = f32[1,16,4096]{2,1,0:T(8,128)S(1)} fusion(f32[16,256]{1,0:T(8,128)S(1)} %psum.14, f32[256,4096]{1,0:T(8,128)} %param.3, s32[4096]{0:T(1024)S(1)} %iota_add_fusion, s32[256]{0:T(256)S(1)} %iota_add_fusion.1), kind=kOutput, calls=%fused_computation.5 | convolution fusion | flops 203423744 | bytes 4490240 | tf_op jit(solution)/shard_map/dot_general | solution.py:31
  61.7 0.0 copy-done
  61.7 2.4 %convolution_bitcast_fusion = f32[1,16,4096]{2,1,0:T(8,128)S(1)} fusion(f32[16,256]{1,0:T(8,128)S(1)} %psum.14, f32[256,4096]{1,0:T(8,128)S(1)} %copy-done, s32[4096]{0:T(1024)S(1)} %iota_add_fusion, s32[256]{0:T(256)S(1)} %iota_add_fusion.1), kind=kOutput, calls=%fused_computation.4 | convolution fusion | flops 203423744 | bytes 4490240 | tf_op jit(solution)/shard_map/dot_general | solution.py:31
  64.1 0.0 copy-done.2
  64.1 0.9 multiply_reduce_fusion
  64.9 0.0 reduce-scatter.2.cloned.1.call-update
  65.0 0.0 copy-start.1
  65.0 5.8 %fusion.14 = f32[1,16,256]{2,1,0:T(8,128)S(1)} fusion(f32[16,4096]{1,0:T(8,128)S(1)} %copy-done.2, f32[256,4096]{1,0:T(8,128)} %param.4, s32[4096]{0:T(1024)S(1)} %iota_add_fusion, s32[256]{0:T(256)S(1)} %iota_add_fusion.1), kind=kOutput, calls=%fused_computation.20 | convolution fusion | flops 203423744 | bytes 4490240 | tf_op jit(solution)/shard_map/dot_general | solution.py:29
  70.7 0.0 copy-done.1
  70.8 3.5 %fusion.15 = f32[1,16,256]{2,1,0:T(8,128)S(1)} fusion(f32[16,4096]{1,0:T(8,128)S(1)} %copy-done.2, f32[256,4096]{1,0:T(8,128)S(1)} %copy-done.1, s32[4096]{0:T(1024)S(1)} %iota_add_fusion, s32[256]{0:T(256)S(1)} %iota_add_fusion.1), kind=kOutput, calls=%fused_computation.21 | convolution fusion | flops 203423744 | bytes 4490240 | tf_op jit(solution)/shard_map/dot_general | solution.py:29
  74.2 0.1 collective-permute-start
  74.3 1.2 collective-permute-done
  75.5 0.1 multiply_reduce_fusion.1
  75.6 5.0 %collective-permute-start.1 = (f32[2,16,256]{2,1,0:T(8,128)S(1)}, f32[2,16,256]{2,1,0:T(8,128)S(1)}, u32[]{:S(2)}, u32[]{:S(2)}) collective-permute-start(f32[2,16,256]{2,1,0:T(8,128)S(1)} %get-tuple-element.6), channel_id=1, source_target_pairs={{0,4},{2,6},{4,0},{6,2},{8,12},{10,14},{12,8},{14,10},{16,20},{18,... | collective-permute-start | bytes 98312 | tf_op jit(solution)/shard_map/ppermute | solution.py:40
  80.6 1.9 %collective-permute-done.1 = f32[2,16,256]{2,1,0:T(8,128)S(1)} collective-permute-done((f32[2,16,256]{2,1,0:T(8,128)S(1)}, f32[2,16,256]{2,1,0:T(8,128)S(1)}, u32[]{:S(2)}, u32[]{:S(2)}) %collective-permute-start.1) | collective-permute-done | bytes 32800 | tf_op jit(solution)/shard_map/ppermute | solution.py:40
  82.5 8.4 %collective-permute-start.2 = (f32[2,16,256]{2,1,0:T(8,128)S(1)}, f32[2,16,256]{2,1,0:T(8,128)S(1)}, u32[]{:S(2)}, u32[]{:S(2)}) collective-permute-start(f32[2,16,256]{2,1,0:T(8,128)S(1)} %add.43), channel_id=1, source_target_pairs={{0,8},{2,10},{4,12},{6,14},{8,0},{10,2},{12,4},{14,6},{16,24},{18,... | collective-permute-start | bytes 98312 | tf_op jit(solution)/shard_map/ppermute | solution.py:40
  90.9 1.9 %collective-permute-done.2 = f32[2,16,256]{2,1,0:T(8,128)S(1)} collective-permute-done((f32[2,16,256]{2,1,0:T(8,128)S(1)}, f32[2,16,256]{2,1,0:T(8,128)S(1)}, u32[]{:S(2)}, u32[]{:S(2)}) %collective-permute-start.2) | collective-permute-done | bytes 32800 | tf_op jit(solution)/shard_map/ppermute | solution.py:40
  92.8 0.6 collective-permute-start.3
  93.5 41.6 %psum.15 = f32[2,16]{1,0:T(2,128)} all-reduce(f32[2,16]{1,0:T(2,128)S(1)} %add.47), channel_id=1, replica_groups=mesh['blk'=16,'grp'=2] {'blk','grp'}, use_global_device_ids=true, to_apply=%region_4.5 | all-reduce | flops 32 | bytes 256 | tf_op jit(solution)/shard_map/psum | solution.py:37
  135.1 0.0 collective-permute-done.3
  135.1 0.6 add.45
  135.7 0.0 reduce-scatter.2.cloned.1.call-done
  (6 shorter events, 0.0 us)
Async XLA Ops:
  7.2 128.5 %reduce-scatter.2.cloned.1.call-start = ((), (), s32[]{:S(2)}) async-start(), calls=%async_computation.1 | async-start | bytes 786432 | tf_op jit(solution)/shard_map/reduce_scatter | solution.py:41
  57.0 4.7 %copy-start = (f32[256,4096]{1,0:T(8,128)S(1)}, f32[256,4096]{1,0:T(8,128)}, u32[]{:S(2)}) copy-start(f32[256,4096]{1,0:T(8,128)} %param.4) | copy-start | bytes 12582916
  57.0 7.1 %copy-start.2 = (f32[16,4096]{1,0:T(8,128)S(1)}, f32[16,4096]{1,0:T(8,128)}, u32[]{:S(2)}) copy-start(f32[16,4096]{1,0:T(8,128)} %param.5) | copy-start | bytes 786436
  65.0 5.8 %copy-start.1 = (f32[256,4096]{1,0:T(8,128)S(1)}, f32[256,4096]{1,0:T(8,128)}, u32[]{:S(2)}) copy-start(f32[256,4096]{1,0:T(8,128)} %param.3) | copy-start | bytes 12582916
  74.2 1.3 collective-permute-start
  75.6 6.9 %collective-permute-start.1 = (f32[2,16,256]{2,1,0:T(8,128)S(1)}, f32[2,16,256]{2,1,0:T(8,128)S(1)}, u32[]{:S(2)}, u32[]{:S(2)}) collective-permute-start(f32[2,16,256]{2,1,0:T(8,128)S(1)} %get-tuple-element.6), channel_id=1, source_target_pairs={{0,4},{2,6},{4,0},{6,2},{8,12},{10,14},{12,8},{14,10},{16,20},{18,... | collective-permute-start | bytes 98312 | tf_op jit(solution)/shard_map/ppermute | solution.py:40
  82.5 10.3 %collective-permute-start.2 = (f32[2,16,256]{2,1,0:T(8,128)S(1)}, f32[2,16,256]{2,1,0:T(8,128)S(1)}, u32[]{:S(2)}, u32[]{:S(2)}) collective-permute-start(f32[2,16,256]{2,1,0:T(8,128)S(1)} %add.43), channel_id=1, source_target_pairs={{0,8},{2,10},{4,12},{6,14},{8,0},{10,2},{12,4},{14,6},{16,24},{18,... | collective-permute-start | bytes 98312 | tf_op jit(solution)/shard_map/ppermute | solution.py:40
  92.8 42.2 %collective-permute-start.3 = (f32[2,16,256]{2,1,0:T(8,128)S(1)}, f32[2,16,256]{2,1,0:T(8,128)S(1)}, u32[]{:S(2)}, u32[]{:S(2)}) collective-permute-start(f32[2,16,256]{2,1,0:T(8,128)S(1)} %add.44), channel_id=1, source_target_pairs={{0,16},{2,18},{4,20},{6,22},{8,24},{10,26},{12,28},{14,30},{16,0},... | collective-permute-start | bytes 98312 | tf_op jit(solution)/shard_map/ppermute | solution.py:40
Sparse Core Ops, SparseCore 0:
  65.1 23.2 reduce-scatter.1

commit v2 on v0

--- a/solution.py
+++ b/solution.py
@@ -34,7 +34,7 @@
     early_local = jnp.sum(slab_probes[None] * direct_terms, axis=2) + jnp.sum(
         probes[None] * mirror_terms, axis=2
     )
-    early_trace = lax.psum(early_local, ("blk", "grp"))
+    early_trace = lax.psum(lax.psum(early_local, "grp"), "blk")
     row_part = lax.psum(direct_terms, "blk")
     column_part = lax.psum_scatter(mirror_terms, "grp", scatter_dimension=2, tiled=True)
     return (row_part, column_part, early_trace)

time: 133 us -> 159 us (1.20)
  the two profiles are of different devices: /device:TPU:14 before, /device:TPU:0 now
where the time goes in v2:
time: 159 us; the launch traced here: 158 us
  blocking collectives  126 us (79%)
  matrix products  16.3 us (10%)
  between operations  14.1 us (9%)
  other arithmetic  1.71 us (1%)
    psum x1, blocking collectives, broadcast(): return lax.psum(block, axis)  63 us
    psum x1, blocking collectives, shards(): row_part = lax.psum(direct_terms, 'blk')  58.3 us
    dot_general x2, matrix products, shards(): lax.dot_general(probes, masked_upper, (((1,), (1,)), ((), ())), precision...  9.23 us
    dot_general x2, matrix products, shards(): mirror_list.append(jnp.dot(slab_probes, masked_strict, precision=hp))  7.08 us
    psum x1, blocking collectives, shards(): early_trace = lax.psum(lax.psum(early_local, 'grp'), 'blk')  4.92 us
  transfers between devices with their start and end apart: 1, of which 0 were waited for; matrix products, arithmetic and copies ran while one was open for 6% of the time, Pallas kernels for 0%

profile of v2, /device:TPU:0, one launch (start us, length us, event | category | flops | bytes accessed | tf_op | source)
XLA Modules:
  0.0 158.3 jit_solution(5963326211020129214)
XLA Ops:
  7.2 0.0 reduce-scatter.2.cloned.1.call-start
  7.2 0.7 dynamic-slice_select_fusion
  8.0 63.0 %psum.29 = f32[16,256]{1,0:T(8,128)S(1)} all-reduce(f32[16,256]{1,0:T(8,128)S(1)} %dynamic-slice_select_fusion), channel_id=1, replica_groups=mesh['blk'=16,'grp'=2] {'blk'}, use_global_device_ids=true, to_apply=%region_1.2 | all-reduce | flops 4096 | bytes 32768 | tf_op jit(solution)/shard_map/psum | solution.py:9
  70.9 0.0 copy-start
  70.9 0.0 copy-start.2
  70.9 4.7 %convolution_bitcast_fusion.1 = f32[1,16,4096]{2,1,0:T(8,128)S(1)} fusion(f32[16,256]{1,0:T(8,128)S(1)} %psum.29, f32[256,4096]{1,0:T(8,128)} %param.3, s32[4096]{0:T(1024)S(1)} %iota_add_fusion, s32[256]{0:T(256)S(1)} %iota_add_fusion.1), kind=kOutput, calls=%fused_computation.5 | convolution fusion | flops 203423744 | bytes 4490240 | tf_op jit(solution)/shard_map/dot_general | solution.py:31
  75.7 0.0 copy-done
  75.7 2.4 %convolution_bitcast_fusion = f32[1,16,4096]{2,1,0:T(8,128)S(1)} fusion(f32[16,256]{1,0:T(8,128)S(1)} %psum.29, f32[256,4096]{1,0:T(8,128)S(1)} %copy-done, s32[4096]{0:T(1024)S(1)} %iota_add_fusion, s32[256]{0:T(256)S(1)} %iota_add_fusion.1), kind=kOutput, calls=%fused_computation.4 | convolution fusion | flops 203423744 | bytes 4490240 | tf_op jit(solution)/shard_map/dot_general | solution.py:31
  78.0 0.0 copy-done.2
  78.0 0.9 pad_maximum_fusion
  78.9 0.0 reduce-scatter.2.cloned.1.call-update
  78.9 0.0 copy-start.1
  78.9 5.8 %fusion.14 = f32[1,16,256]{2,1,0:T(8,128)S(1)} fusion(f32[16,4096]{1,0:T(8,128)S(1)} %copy-done.2, f32[256,4096]{1,0:T(8,128)} %param.4, s32[4096]{0:T(1024)S(1)} %iota_add_fusion, s32[256]{0:T(256)S(1)} %iota_add_fusion.1), kind=kOutput, calls=%fused_computation.20 | convolution fusion | flops 203423744 | bytes 4490240 | tf_op jit(solution)/shard_map/dot_general | solution.py:29
  84.7 0.0 copy-done.1
  84.7 3.5 %fusion.15 = f32[1,16,256]{2,1,0:T(8,128)S(1)} fusion(f32[16,4096]{1,0:T(8,128)S(1)} %copy-done.2, f32[256,4096]{1,0:T(8,128)S(1)} %copy-done.1, s32[4096]{0:T(1024)S(1)} %iota_add_fusion, s32[256]{0:T(256)S(1)} %iota_add_fusion.1), kind=kOutput, calls=%fused_computation.21 | convolution fusion | flops 203423744 | bytes 4490240 | tf_op jit(solution)/shard_map/dot_general | solution.py:29
  88.2 0.1 multiply_reduce_fusion.1
  88.3 4.9 %psum.30 = f32[2,16]{1,0:T(2,128)S(1)} all-reduce(f32[2,16]{1,0:T(2,128)S(1)} %add.35), channel_id=1, replica_groups=mesh['blk'=16,'grp'=2] {'grp'}, use_global_device_ids=true, to_apply=%region_5.6 | all-reduce | flops 32 | bytes 256 | tf_op jit(solution)/shard_map/psum | solution.py:37
  93.2 58.3 %all-reduce = (f32[2,16,256]{2,1,0:T(8,128)}, f32[2,16]{1,0:T(2,128)}) all-reduce(f32[2,16,256]{2,1,0:T(8,128)S(1)} %get-tuple-element.8, f32[2,16]{1,0:T(2,128)S(1)} %psum.30), channel_id=1, replica_groups=mesh['blk'=16,'grp'=2] {'blk'}, use_global_device_ids=true, to_apply=%region_0.1 | all-reduce | flops 8224 | bytes 65792 | tf_op jit(solution)/shard_map/psum | solution.py:38
  151.5 0.0 reduce-scatter.2.cloned.1.call-done
  (3 shorter events, 0.0 us)
Async XLA Ops:
  7.2 144.3 %reduce-scatter.2.cloned.1.call-start = ((), (), s32[]{:S(2)}) async-start(), calls=%async_computation.1 | async-start | bytes 786432 | tf_op jit(solution)/shard_map/reduce_scatter | solution.py:39
  70.9 4.7 %copy-start = (f32[256,4096]{1,0:T(8,128)S(1)}, f32[256,4096]{1,0:T(8,128)}, u32[]{:S(2)}) copy-start(f32[256,4096]{1,0:T(8,128)} %param.4) | copy-start | bytes 12582916
  70.9 7.1 %copy-start.2 = (f32[16,4096]{1,0:T(8,128)S(1)}, f32[16,4096]{1,0:T(8,128)}, u32[]{:S(2)}) copy-start(f32[16,4096]{1,0:T(8,128)} %param.5) | copy-start | bytes 786436
  78.9 5.8 %copy-start.1 = (f32[256,4096]{1,0:T(8,128)S(1)}, f32[256,4096]{1,0:T(8,128)}, u32[]{:S(2)}) copy-start(f32[256,4096]{1,0:T(8,128)} %param.3) | copy-start | bytes 12582916
Sparse Core Ops, SparseCore 0:
  79.0 11.9 reduce-scatter.1
